TPU v7x, 32 devices: a whole 2x2x4 slice. The times are simulated.
32 devices in a mesh: rows: 4 (over x, core), cols: 8 (over z, y).
Axes of the slice: x: 2, y: 2, z: 4, core: 2. Of those that a mesh axis runs over, the one named last changes fastest.
Arguments:
- samples: bfloat16 [2048, 65536], P('rows', 'cols'), may hold values from -0.0234375 to 0.0234375
- labels: int32 [2048], P('rows'), may hold values 0 or 1
- weights: float32 [65536], P('cols'), may hold values from -7 to 7, as said below
- hist_s: float32 [16, 65536], P(None, 'cols'), may hold values from -60 to 60
- hist_y: float32 [16, 65536], P(None, 'cols'), may hold values from -480 to 480, as said below
- counter: int32 [1], replicated, may hold values from 0 to 4095
Outputs:
- new_weights: float32 [65536], P('cols')
- gradient: float32 [65536], P('cols')
Inputs may be any that keep to these rules, and one draw needn't show every extreme that they name: weights share a common direction with the rows of hist_s. Each entry of hist_y[j] is a positive multiple of the same entry of hist_s[j], so s_j . y_j > 0.
All inputs are finite; a program needn't handle non-finite values. No bound on the sum of `labels` on one device may be relied on, other than what follows from the above.
Results may differ from a plain program's by a relative error of at most 0.0013.
Values sent between devices are 32-bit elements; how exact they have to be, the bound alone decides.
A program may use at most 64 MiB of HBM per device.

v0:
```python
import jax
import jax.numpy as jnp
from jax import lax
from jax.sharding import PartitionSpec as P

HIST = 16
penalty = 4.0
step_length = 0.5
highest = lax.Precision.HIGHEST


def row_share(values):
    width = values.shape[-1] // lax.axis_size("rows")
    return lax.dynamic_slice_in_dim(values, lax.axis_index("rows") * width, width, values.ndim - 1)


def quad_form(left, matrix, right):
    return jnp.dot(left, jnp.dot(matrix, right, precision=highest), precision=highest)


def gram_recursion(gram, basis, newest):
    count = 2 * HIST + 1
    places = jnp.arange(count, dtype=jnp.int32)
    select_s = (places == newest).astype(jnp.float32)
    select_y = (places == newest + HIST).astype(jnp.float32)
    gamma = quad_form(select_s, gram, select_y) / quad_form(select_y, gram, select_y)
    weights_of = (places == 2 * HIST).astype(jnp.float32)
    coefs = []
    pairs = []
    for step in range(HIST):
        slot = (newest - step) % HIST
        pick_s = (places == slot).astype(jnp.float32)
        pick_y = (places == slot + HIST).astype(jnp.float32)
        rho = 1.0 / quad_form(pick_s, gram, pick_y)
        coef = rho * quad_form(pick_s, gram, weights_of)
        coefs.append(coef)
        pairs.append((pick_s, pick_y, rho))
        weights_of = weights_of - coef * pick_y
    result_of = gamma * weights_of
    for step in reversed(range(HIST)):
        pick_s, pick_y, rho = pairs[step]
        beta = rho * quad_form(pick_y, gram, result_of)
        result_of = result_of + (coefs[step] - beta) * pick_s
    return jnp.dot(result_of, basis, precision=highest)


def body(samples, labels, weights, hist_s, hist_y, counter):
    margin_part = jnp.dot(samples, weights.astype(jnp.bfloat16), preferred_element_type=jnp.float32)
    margin = lax.psum(margin_part, "cols")
    resid = (jax.nn.sigmoid(margin) - labels.astype(jnp.float32)).astype(jnp.bfloat16)
    total_part = jnp.dot(resid, samples, preferred_element_type=jnp.float32)
    newest = counter[0] % HIST
    total = lax.psum(total_part, "rows")
    gradient = weights + penalty * total
    basis = jnp.concatenate([hist_s, hist_y, gradient[None, :]], axis=0)
    narrow_basis = row_share(basis)
    gram_part = jnp.dot(
        narrow_basis, narrow_basis.T, precision=highest, preferred_element_type=jnp.float32
    )
    gram = lax.psum(gram_part, ("rows", "cols"))
    result = gram_recursion(gram, basis, newest)
    return (weights - step_length * result, gradient)


def solution(mesh):
    in_specs = (P("rows", "cols"), P("rows"), P("cols"), P(None, "cols"), P(None, "cols"), P())
    out_specs = (P("cols"), P("cols"))
    return jax.shard_map(body, mesh=mesh, in_specs=in_specs, out_specs=out_specs, check_vma=False)
```

profile of v0, /device:TPU:14, one launch (start us, length us, event | category | flops | bytes accessed | tf_op | source)
XLA Modules:
  0.0 156.8 jit_solution(8693725162735482173)
XLA Ops:
  0.6 0.8 convert_element_type.8
  1.4 5.6 %fusion.186 = f32[1,512]{1,0:T(1,128)S(1)} fusion(bf16[512,8192]{1,0:T(8,128)(2,1)} %param.6, bf16[8192,1]{0,1:T(2,128)(2,1)S(1)} %reshape.4), kind=kOutput, calls=%fused_computation.303 | convolution fusion | flops 8388608 | bytes 8407040 | tf_op jit(solution)/shard_map/dot_general | solution.py:48
  7.1 15.2 %psum.21 = f32[512]{0:T(512)S(1)} all-reduce(f32[512]{0:T(512)S(1)} %bitcast.507), channel_id=1, replica_groups=mesh['rows'=4,'cols'=8] {'cols'}, use_global_device_ids=true, to_apply=%region_0.0 | all-reduce | flops 512 | bytes 4096 | tf_op jit(solution)/shard_map/psum | solution.py:49
  22.3 4.7 %fusion.187 = f32[1,8192]{1,0:T(1,128)S(1)} fusion(bf16[512,1]{0,1:T(2,128)(2,1)S(1)} %reshape.6, bf16[512,8192]{1,0:T(8,128)(2,1)} %param.6), kind=kOutput, calls=%fused_computation.304 | convolution fusion | flops 8388608 | bytes 8422400 | tf_op jit(solution)/shard_map/dot_general | solution.py:51
  26.9 10.4 %psum.22 = f32[8192]{0:T(1024)S(1)} all-reduce(f32[8192]{0:T(1024)S(1)} %bitcast.505), channel_id=1, replica_groups=mesh['rows'=4,'cols'=8] {'rows'}, use_global_device_ids=true, to_apply=%region_1.2 | all-reduce | flops 8192 | bytes 65536 | tf_op jit(solution)/shard_map/psum | solution.py:53
  37.9 45.6 %psum.23 = f32[33,33]{1,0:T(8,128)S(1)} all-reduce(f32[33,33]{1,0:T(8,128)S(1)} %fusion.96), channel_id=1, replica_groups=mesh['rows'=4,'cols'=8] {'rows','cols'}, use_global_device_ids=true, to_apply=%region_2.3 | all-reduce | flops 1089 | bytes 8712 | tf_op jit(solution)/shard_map/psum | solution.py:60
  85.7 0.7 fusion.49
  87.1 0.7 fusion.50
  88.5 0.8 fusion.51
  90.0 0.7 fusion.52
  91.4 0.8 fusion.53
  92.8 0.7 fusion.56
  94.3 0.7 fusion.54
  95.7 0.8 fusion.55
  97.1 0.8 fusion.57
  98.6 0.7 fusion.60
  100.0 0.7 fusion.58
  101.5 0.8 fusion.59
  102.9 0.8 fusion.61
  107.2 0.8 fusion.63
  108.6 0.8 fusion.65
  110.1 0.7 fusion.68
  111.5 0.7 fusion.66
  113.0 0.8 fusion.67
  114.4 0.8 fusion.69
  115.8 0.7 fusion.72
  118.7 0.8 fusion.71
  120.1 0.8 fusion.73
  124.5 0.8 fusion.75
  125.9 0.8 fusion.77
  128.8 0.8 fusion.79
  130.2 0.8 fusion.121
  132.4 0.8 fusion.80
  133.8 0.8 fusion.81
  135.3 0.8 fusion.82
  136.7 0.8 fusion.83
  138.2 0.8 fusion.84
  139.6 0.8 fusion.85
  141.1 0.8 fusion.86
  142.5 0.8 fusion.87
  144.0 0.8 fusion.88
  145.4 0.8 fusion.89
  146.9 0.8 fusion.90
  148.3 0.8 fusion.91
  149.8 0.8 fusion.92
  151.2 0.8 fusion.93
  152.6 0.8 fusion.94
  154.0 0.8 fusion.95
  (39 shorter events, 7.7 us)
Async XLA Ops:
  1.4 20.8 %copy-start.4 = (s32[512]{0:T(512)S(1)}, s32[512]{0:T(512)}, u32[]{:S(2)}) copy-start(s32[512]{0:T(512)} %param.7) | copy-start | bytes 6148
  22.2 15.1 %copy-start.2 = (f32[8192]{0:T(1024)S(1)}, f32[8192]{0:T(1024)}, u32[]{:S(2)}) copy-start(f32[8192]{0:T(1024)} %param.8) | copy-start | bytes 98308
  22.3 15.1 %copy-start = (f32[16,8192]{1,0:T(8,128)S(1)}, f32[16,8192]{1,0:T(8,128)}, u32[]{:S(2)}) copy-start(f32[16,8192]{1,0:T(8,128)} %param.10) | copy-start | bytes 1572868
  22.3 15.1 %copy-start.1 = (f32[16,8192]{1,0:T(8,128)S(1)}, f32[16,8192]{1,0:T(8,128)}, u32[]{:S(2)}) copy-start(f32[16,8192]{1,0:T(8,128)} %param.9) | copy-start | bytes 1572868
  37.4 118.1 %copy-start.3 = (f32[8192]{0:T(1024)}, f32[8192]{0:T(1024)S(1)}, u32[]{:S(2)}) copy-start(f32[8192]{0:T(1024)S(1)} %multiply_add_fusion) | copy-start | bytes 98308
where the time goes:
time: 158 us; the launch traced here: 157 us
  blocking collectives  71.2 us (45%)
  matrix products  48.3 us (31%)
  between operations  35.2 us (22%)
  other arithmetic  2.05 us (1%)
    psum x1, blocking collectives, body(): gram = lax.psum(gram_part, ('rows', 'cols'))  45.6 us
    dot_general x49, matrix products, quad_form(): jnp.dot(matrix, right, precision=highest)  36.8 us
    psum x1, blocking collectives, body(): margin = lax.psum(margin_part, 'cols')  15.2 us
    psum x1, blocking collectives, body(): total = lax.psum(total_part, 'rows')  10.4 us
    dot_general x1, matrix products, body(): jnp.dot(samples, weights.astype(jnp.bfloat16), preferred_element_type=jnp...  5.64 us
    dot_general x1, matrix products, body(): total_part = jnp.dot(resid, samples, preferred_element_type=jnp.float32)  4.66 us

commit v1 on v0

--- a/solution.py
+++ b/solution.py
@@ -46,7 +46,9 @@
 
 def body(samples, labels, weights, hist_s, hist_y, counter):
     margin_part = jnp.dot(samples, weights.astype(jnp.bfloat16), preferred_element_type=jnp.float32)
-    margin = lax.psum(margin_part, "cols")
+    margin = margin_part
+    for hop in (1, 2, 4):
+        margin = margin + lax.ppermute(margin, "cols", [(dev, dev ^ hop) for dev in range(8)])
     resid = (jax.nn.sigmoid(margin) - labels.astype(jnp.float32)).astype(jnp.bfloat16)
     total_part = jnp.dot(resid, samples, preferred_element_type=jnp.float32)
     newest = counter[0] % HIST

time: 158 us -> 151 us (0.956)
  blocking collectives: 71.2 us -> 50.8 us
  waiting for transfers between devices: 0 us -> 7.24 us
  starting transfers between devices: 0 us -> 3.56 us
    psum x1 -> x0, blocking collectives: 15.2 us -> none  [body(): margin = lax.psum(margin_part, 'cols')]
    ppermute x0 -> x3, waiting for transfers between devices: none -> 7.24 us  [body(): lax.ppermute(margin, 'cols', [(dev, dev ^ hop) for dev in range(8)])]
    psum x1, blocking collectives: 45.6 us -> 40.4 us  [body(): gram = lax.psum(gram_part, ('rows', 'cols'))]
    ppermute x0 -> x3, starting transfers between devices: none -> 3.56 us  [body(): lax.ppermute(margin, 'cols', [(dev, dev ^ hop) for dev in range(8)])]
  transfers between devices with their start and end apart: 0 -> 3, of which waited for: 0 -> 3; matrix products, arithmetic and copies ran while one was open for 0% -> 0% of each run, Pallas kernels for 0% -> 0%
where the time goes in v1:
time: 151 us; the launch traced here: 149 us
  blocking collectives  50.8 us (34%)
  matrix products  49.5 us (33%)
  between operations  35.5 us (24%)
  waiting for transfers between devices  7.24 us (5%)
  starting transfers between devices  3.56 us (2%)
  other arithmetic  2.06 us (1%)
    psum x1, blocking collectives, body(): gram = lax.psum(gram_part, ('rows', 'cols'))  40.4 us
    dot_general x49, matrix products, quad_form(): jnp.dot(matrix, right, precision=highest)  38 us
    psum x1, blocking collectives, body(): total = lax.psum(total_part, 'rows')  10.4 us
    ppermute x3, waiting for transfers between devices, body(): lax.ppermute(margin, 'cols', [(dev, dev ^ hop) for dev in range(8)])  7.24 us
    dot_general x1, matrix products, body(): jnp.dot(samples, weights.astype(jnp.bfloat16), preferred_element_type=jnp...  5.64 us
    dot_general x1, matrix products, body(): total_part = jnp.dot(resid, samples, preferred_element_type=jnp.float32)  4.66 us
    ppermute x3, starting transfers between devices, body(): lax.ppermute(margin, 'cols', [(dev, dev ^ hop) for dev in range(8)])  3.56 us
  transfers between devices with their start and end apart: 3, of which 3 were waited for; matrix products, arithmetic and copies ran while one was open for 0% of the time, Pallas kernels for 0%

profile of v1, /device:TPU:14, one launch (start us, length us, event | category | flops | bytes accessed | tf_op | source)
XLA Modules:
  0.0 148.7 jit_solution(17330167757967100074)
XLA Ops:
  0.6 0.8 convert_element_type.8
  1.4 5.6 %fusion.186 = f32[1,512]{1,0:T(1,128)S(1)} fusion(bf16[512,8192]{1,0:T(8,128)(2,1)} %param.6, bf16[8192,1]{0,1:T(2,128)(2,1)S(1)} %reshape.4), kind=kOutput, calls=%fused_computation.303 | convolution fusion | flops 8388608 | bytes 8407040 | tf_op jit(solution)/shard_map/dot_general | solution.py:48
  8.5 2.2 %collective-permute-done = f32[512]{0:T(512)S(1)} collective-permute-done((f32[512]{0:T(512)S(1)}, f32[512]{0:T(512)S(1)}, u32[]{:S(2)}, u32[]{:S(2)}) %collective-permute-start) | collective-permute-done | bytes 2080 | tf_op jit(solution)/shard_map/ppermute | solution.py:51
  11.1 3.1 %collective-permute-done.1 = f32[512]{0:T(512)S(1)} collective-permute-done((f32[512]{0:T(512)S(1)}, f32[512]{0:T(512)S(1)}, u32[]{:S(2)}, u32[]{:S(2)}) %collective-permute-start.1) | collective-permute-done | bytes 2080 | tf_op jit(solution)/shard_map/ppermute | solution.py:51
  14.3 2.6 %collective-permute-start.2 = (f32[512]{0:T(512)S(1)}, f32[512]{0:T(512)S(1)}, u32[]{:S(2)}, u32[]{:S(2)}) collective-permute-start(f32[512]{0:T(512)S(1)} %add.190), channel_id=1, source_target_pairs={{0,4},{1,5},{2,6},{3,7},{4,0},{5,1},{6,2},{7,3},{8,12},{9,13},{10,... | collective-permute-start | bytes 6152 | tf_op jit(solution)/shard_map/ppermute | solution.py:51
  16.9 1.9 %collective-permute-done.2 = f32[512]{0:T(512)S(1)} collective-permute-done((f32[512]{0:T(512)S(1)}, f32[512]{0:T(512)S(1)}, u32[]{:S(2)}, u32[]{:S(2)}) %collective-permute-start.2) | collective-permute-done | bytes 2080 | tf_op jit(solution)/shard_map/ppermute | solution.py:51
  18.8 4.7 %fusion.187 = f32[1,8192]{1,0:T(1,128)S(1)} fusion(bf16[512,1]{0,1:T(2,128)(2,1)S(1)} %reshape.6, bf16[512,8192]{1,0:T(8,128)(2,1)} %param.6), kind=kOutput, calls=%fused_computation.304 | convolution fusion | flops 8388608 | bytes 8422400 | tf_op jit(solution)/shard_map/dot_general | solution.py:53
  23.5 10.4 %psum.14 = f32[8192]{0:T(1024)S(1)} all-reduce(f32[8192]{0:T(1024)S(1)} %bitcast.505), channel_id=1, replica_groups=mesh['rows'=4,'cols'=8] {'rows'}, use_global_device_ids=true, to_apply=%region_0.1 | all-reduce | flops 8192 | bytes 65536 | tf_op jit(solution)/shard_map/psum | solution.py:55
  34.5 40.4 %psum.15 = f32[33,33]{1,0:T(8,128)S(1)} all-reduce(f32[33,33]{1,0:T(8,128)S(1)} %fusion.96), channel_id=1, replica_groups=mesh['rows'=4,'cols'=8] {'rows','cols'}, use_global_device_ids=true, to_apply=%region_1.2 | all-reduce | flops 1089 | bytes 8712 | tf_op jit(solution)/shard_map/psum | solution.py:62
  74.9 0.8 fusion.49
  79.9 0.8 fusion.52
  82.1 0.8 fusion.53
  82.9 0.8 fusion.56
  84.5 0.8 fusion.54
  88.1 0.8 fusion.57
  88.8 0.8 fusion.60
  90.4 0.8 fusion.58
  94.0 0.8 fusion.61
  94.8 0.8 fusion.64
  96.3 0.8 fusion.62
  98.6 0.8 fusion.63
  100.0 0.8 fusion.65
  100.7 0.8 fusion.68
  102.3 0.8 fusion.66
  104.5 0.8 fusion.67
  105.9 0.8 fusion.69
  106.7 0.8 fusion.72
  108.2 0.8 fusion.70
  111.9 0.8 fusion.73
  112.6 0.8 fusion.76
  114.2 0.8 fusion.74
  116.4 0.8 fusion.75
  117.8 0.8 fusion.77
  118.6 0.8 fusion.78
  121.6 0.8 fusion.121
  124.4 0.8 fusion.80
  125.8 0.8 fusion.81
  127.3 0.8 fusion.82
  128.7 0.8 fusion.83
  130.1 0.8 fusion.84
  131.6 0.8 fusion.85
  133.0 0.8 fusion.86
  134.4 0.8 fusion.87
  135.9 0.8 fusion.88
  137.3 0.8 fusion.89
  138.8 0.8 fusion.90
  141.7 0.8 fusion.92
  143.1 0.8 fusion.93
  (46 shorter events, 11.0 us)
Async XLA Ops:
  1.4 17.3 %copy-start.4 = (s32[512]{0:T(512)S(1)}, s32[512]{0:T(512)}, u32[]{:S(2)}) copy-start(s32[512]{0:T(512)} %param.7) | copy-start | bytes 6148
  7.1 3.6 %collective-permute-start = (f32[512]{0:T(512)S(1)}, f32[512]{0:T(512)S(1)}, u32[]{:S(2)}, u32[]{:S(2)}) collective-permute-start(f32[512]{0:T(512)S(1)} %bitcast.507), channel_id=1, source_target_pairs={{0,1},{1,0},{2,3},{3,2},{4,5},{5,4},{6,7},{7,6},{8,9},{9,8},{10,11... | collective-permute-start | bytes 6152 | tf_op jit(solution)/shard_map/ppermute | solution.py:51
  10.7 3.6 %collective-permute-start.1 = (f32[512]{0:T(512)S(1)}, f32[512]{0:T(512)S(1)}, u32[]{:S(2)}, u32[]{:S(2)}) collective-permute-start(f32[512]{0:T(512)S(1)} %add.189), channel_id=1, source_target_pairs={{0,2},{1,3},{2,0},{3,1},{4,6},{5,7},{6,4},{7,5},{8,10},{9,11},{10,... | collective-permute-start | bytes 6152 | tf_op jit(solution)/shard_map/ppermute | solution.py:51
  14.3 4.5 %collective-permute-start.2 = (f32[512]{0:T(512)S(1)}, f32[512]{0:T(512)S(1)}, u32[]{:S(2)}, u32[]{:S(2)}) collective-permute-start(f32[512]{0:T(512)S(1)} %add.190), channel_id=1, source_target_pairs={{0,4},{1,5},{2,6},{3,7},{4,0},{5,1},{6,2},{7,3},{8,12},{9,13},{10,... | collective-permute-start | bytes 6152 | tf_op jit(solution)/shard_map/ppermute | solution.py:51
  18.8 15.1 %copy-start.2 = (f32[8192]{0:T(1024)S(1)}, f32[8192]{0:T(1024)}, u32[]{:S(2)}) copy-start(f32[8192]{0:T(1024)} %param.8) | copy-start | bytes 98308
  18.8 15.1 %copy-start = (f32[16,8192]{1,0:T(8,128)S(1)}, f32[16,8192]{1,0:T(8,128)}, u32[]{:S(2)}) copy-start(f32[16,8192]{1,0:T(8,128)} %param.10) | copy-start | bytes 1572868
  18.8 15.1 %copy-start.1 = (f32[16,8192]{1,0:T(8,128)S(1)}, f32[16,8192]{1,0:T(8,128)}, u32[]{:S(2)}) copy-start(f32[16,8192]{1,0:T(8,128)} %param.9) | copy-start | bytes 1572868
  33.9 113.5 %copy-start.3 = (f32[8192]{0:T(1024)}, f32[8192]{0:T(1024)S(1)}, u32[]{:S(2)}) copy-start(f32[8192]{0:T(1024)S(1)} %multiply_add_fusion) | copy-start | bytes 98308

commit v2 on v0

--- a/solution.py
+++ b/solution.py
@@ -57,7 +57,7 @@
     gram_part = jnp.dot(
         narrow_basis, narrow_basis.T, precision=highest, preferred_element_type=jnp.float32
     )
-    gram = lax.psum(gram_part, ("rows", "cols"))
+    gram = lax.psum(lax.psum(gram_part, "cols"), "rows")
     result = gram_recursion(gram, basis, newest)
     return (weights - step_length * result, gradient)
 

time: 158 us -> 163 us (1.032)
  the two profiles are of different devices: /device:TPU:14 before, /device:TPU:0 now
where the time goes in v2:
time: 163 us; the launch traced here: 162 us
  blocking collectives  76.7 us (47%)
  matrix products  48.3 us (30%)
  between operations  35.2 us (22%)
  other arithmetic  2.05 us (1%)
    psum x2, blocking collectives, body(): gram = lax.psum(lax.psum(gram_part, 'cols'), 'rows')  43.3 us
    dot_general x49, matrix products, quad_form(): jnp.dot(matrix, right, precision=highest)  36.8 us
    psum x1, blocking collectives, body(): margin = lax.psum(margin_part, 'cols')  23.1 us
    psum x1, blocking collectives, body(): total = lax.psum(total_part, 'rows')  10.3 us
    dot_general x1, matrix products, body(): jnp.dot(samples, weights.astype(jnp.bfloat16), preferred_element_type=jnp...  5.64 us
    dot_general x1, matrix products, body(): total_part = jnp.dot(resid, samples, preferred_element_type=jnp.float32)  4.66 us

profile of v2, /device:TPU:0, one launch (start us, length us, event | category | flops | bytes accessed | tf_op | source)
XLA Modules:
  0.0 162.3 jit_solution(14291415026281240174)
XLA Ops:
  0.6 0.8 convert_element_type.8
  1.4 5.6 %fusion.186 = f32[1,512]{1,0:T(1,128)S(1)} fusion(bf16[512,8192]{1,0:T(8,128)(2,1)} %param.6, bf16[8192,1]{0,1:T(2,128)(2,1)S(1)} %reshape.4), kind=kOutput, calls=%fused_computation.303 | convolution fusion | flops 8388608 | bytes 8407040 | tf_op jit(solution)/shard_map/dot_general | solution.py:48
  7.1 23.1 %psum.28 = f32[512]{0:T(512)S(1)} all-reduce(f32[512]{0:T(512)S(1)} %bitcast.507), channel_id=1, replica_groups=mesh['rows'=4,'cols'=8] {'cols'}, use_global_device_ids=true, to_apply=%region_0.0 | all-reduce | flops 512 | bytes 4096 | tf_op jit(solution)/shard_map/psum | solution.py:49
  30.3 4.7 %fusion.187 = f32[1,8192]{1,0:T(1,128)S(1)} fusion(bf16[512,1]{0,1:T(2,128)(2,1)S(1)} %reshape.6, bf16[512,8192]{1,0:T(8,128)(2,1)} %param.6), kind=kOutput, calls=%fused_computation.304 | convolution fusion | flops 8388608 | bytes 8422400 | tf_op jit(solution)/shard_map/dot_general | solution.py:51
  34.9 10.3 %psum.29 = f32[8192]{0:T(1024)S(1)} all-reduce(f32[8192]{0:T(1024)S(1)} %bitcast.505), channel_id=1, replica_groups=mesh['rows'=4,'cols'=8] {'rows'}, use_global_device_ids=true, to_apply=%region_1.2 | all-reduce | flops 8192 | bytes 65536 | tf_op jit(solution)/shard_map/psum | solution.py:53
  45.8 33.0 %psum.30 = f32[33,33]{1,0:T(8,128)S(1)} all-reduce(f32[33,33]{1,0:T(8,128)S(1)} %fusion.96), channel_id=1, replica_groups=mesh['rows'=4,'cols'=8] {'cols'}, use_global_device_ids=true, to_apply=%region_2.3 | all-reduce | flops 1089 | bytes 8712 | tf_op jit(solution)/shard_map/psum | solution.py:60
  78.8 10.2 %psum.31 = f32[33,33]{1,0:T(8,128)S(1)} all-reduce(f32[33,33]{1,0:T(8,128)S(1)} %psum.30), channel_id=1, replica_groups=mesh['rows'=4,'cols'=8] {'rows'}, use_global_device_ids=true, to_apply=%region_3.4 | all-reduce | flops 1089 | bytes 8712 | tf_op jit(solution)/shard_map/psum | solution.py:60
  89.7 0.7 fusion.48
  91.2 0.7 fusion.49
  94.0 0.8 fusion.51
  96.9 0.8 fusion.53
  98.3 0.7 fusion.56
  101.2 0.8 fusion.55
  102.6 0.8 fusion.57
  104.1 0.7 fusion.60
  107.0 0.8 fusion.59
  108.4 0.8 fusion.61
  109.8 0.7 fusion.64
  111.3 0.7 fusion.62
  112.7 0.8 fusion.63
  114.1 0.8 fusion.65
  115.6 0.7 fusion.68
  118.5 0.8 fusion.67
  119.9 0.8 fusion.69
  121.3 0.7 fusion.72
  124.2 0.8 fusion.71
  125.6 0.8 fusion.73
  127.1 0.7 fusion.76
  130.0 0.8 fusion.75
  131.4 0.8 fusion.77
  134.3 0.8 fusion.79
  135.7 0.8 fusion.121
  137.9 0.8 fusion.80
  139.3 0.8 fusion.81
  140.8 0.8 fusion.82
  142.2 0.8 fusion.83
  143.7 0.8 fusion.84
  145.1 0.8 fusion.85
  146.6 0.8 fusion.86
  148.0 0.8 fusion.87
  149.5 0.8 fusion.88
  150.9 0.8 fusion.89
  152.4 0.8 fusion.90
  153.8 0.8 fusion.91
  155.3 0.8 fusion.92
  156.7 0.8 fusion.93
  158.1 0.8 fusion.94
  159.5 0.8 fusion.95
  (40 shorter events, 8.4 us)
Async XLA Ops:
  1.4 28.8 %copy-start.4 = (s32[512]{0:T(512)S(1)}, s32[512]{0:T(512)}, u32[]{:S(2)}) copy-start(s32[512]{0:T(512)} %param.7) | copy-start | bytes 6148
  30.2 15.0 %copy-start.2 = (f32[8192]{0:T(1024)S(1)}, f32[8192]{0:T(1024)}, u32[]{:S(2)}) copy-start(f32[8192]{0:T(1024)} %param.8) | copy-start | bytes 98308
  30.3 15.0 %copy-start = (f32[16,8192]{1,0:T(8,128)S(1)}, f32[16,8192]{1,0:T(8,128)}, u32[]{:S(2)}) copy-start(f32[16,8192]{1,0:T(8,128)} %param.10) | copy-start | bytes 1572868
  30.3 15.0 %copy-start.1 = (f32[16,8192]{1,0:T(8,128)S(1)}, f32[16,8192]{1,0:T(8,128)}, u32[]{:S(2)}) copy-start(f32[16,8192]{1,0:T(8,128)} %param.9) | copy-start | bytes 1572868
  45.2 115.7 %copy-start.3 = (f32[8192]{0:T(1024)}, f32[8192]{0:T(1024)S(1)}, u32[]{:S(2)}) copy-start(f32[8192]{0:T(1024)S(1)} %multiply_add_fusion) | copy-start | bytes 98308
